TPU v7x, 256 devices: a whole 4x4x8 slice. The times are simulated.
256 devices in a mesh: dp: 32 (over x, y, core), tensor: 8 (over z).
Axes of the slice: x: 4, y: 4, z: 8, core: 2. Of those that a mesh axis runs over, the one named last changes fastest.
Arguments:
- proxy_hidden: bfloat16 [1536, 4096], P('dp', 'tensor'), may hold values from -176.625 to 176.625
- reference_hidden: bfloat16 [1536, 4096], P('dp', 'tensor'), may hold values from -176.625 to 176.625
- proxy_head: bfloat16 [128256, 4096], P(('dp', 'tensor')), may hold values from -0.09375 to 0.09375
- reference_head: bfloat16 [128256, 4096], P(('dp', 'tensor')), may hold values from -0.09375 to 0.09375
- targets: int32 [1536], P('dp'), may hold values from 0 to 128255
- domains: int32 [1536], P('dp'), may hold values from 0 to 127
- keep_mask: int32 [1536], P('dp'), may hold values 0 or 1
- prior_weights: float32 [128], replicated, may hold values from 0.5 to 2
Outputs:
- excess: float32 [1536], P('dp')
- log_weights: float32 [128], replicated
All inputs are finite; a program needn't handle non-finite values. No bound on the sum of `keep_mask` on one device may be relied on, other than what follows from the above.
Results may differ from a plain program's by a relative error of at most 0.00045.
Values may be sent and summed in bfloat16 or wider, within the bound.
A program may use at most 128 MiB of HBM per device.

v0:
```python
import jax
import jax.numpy as jnp
from jax import lax
from jax.sharding import Mesh
from jax.sharding import PartitionSpec as P

DOMAINS = 128
STEPS = 3
DP = ("dp_0", "dp_1", "dp_2")
DP_TENSOR = ("dp_0", "dp_1", "dp_2", "tensor")
step_size = 1.0
smoothing = 0.001


def gather_turned(arrays, axis, dims):
    turned = [jnp.moveaxis(a, dim, 0) for a, dim in zip(arrays, dims)]
    widths = [t[0].size for t in turned]
    both = jnp.concatenate([t.reshape(-1, w) for t, w in zip(turned, widths)], axis=1)
    whole = lax.all_gather(both, axis, axis=0, tiled=True)
    pieces = jnp.split(whole, [sum(widths[:k]) for k in range(1, len(widths))], axis=1)
    return tuple(
        (
            jnp.moveaxis(b.reshape(-1, *t.shape[1:]), 0, dim)
            for b, t, dim in zip(pieces, turned, dims)
        )
    )


def copy_for_each(array, axis):
    copies = jnp.broadcast_to(array, (lax.axis_size(axis), *array.shape))
    return lax.all_to_all(copies, axis, split_axis=0, concat_axis=0, tiled=True)


def in_order(pieces, dim):
    dims = list(pieces.shape[1:])
    dims[dim] *= pieces.shape[0]
    return jnp.moveaxis(pieces, 0, dim).reshape(dims)


def gather_directly(array, axis, dim):
    pieces = copy_for_each(array, axis)
    return in_order(pieces, dim)


def all_in_one(array, axis):
    leaves = jax.tree.leaves(array)
    turns = sorted(range(len(leaves)), key=lambda k: -leaves[k].size)
    width = (1, *leaves[turns[0]].shape)[-1]
    lines = [
        jnp.pad(leaves[k].reshape(-1), (0, -leaves[k].size % width)).reshape(-1, width)
        for k in turns
    ]
    both, at, found = (lax.all_gather(jnp.concatenate(lines), axis), 0, {})
    for k, line in zip(turns, lines):
        share = both[:, at : at + len(line)].reshape(len(both), -1)
        found[k] = share[:, : leaves[k].size].reshape(-1, *leaves[k].shape)
        at += len(line)
    numbers = iter(range(len(leaves)))
    return jax.tree.map(lambda _: found[next(numbers)], array)


def combined_by_axis(array, axes, combine):
    for axis in axes:
        pieces = all_in_one(array, axis)
        array = jax.tree.map(lambda part: part[0], pieces)
        for k in range(1, lax.axis_size(axis)):
            array = combine(array, jax.tree.map(lambda part: part[k], pieces))
    return array


def project(rows, head):
    return lax.dot_general(rows, head, (((1,), (1,)), ((), ())), preferred_element_type=jnp.float32)


def row_stats(logits, wanted):
    columns = jnp.arange(logits.shape[1], dtype=jnp.int32)
    row_peak = jnp.max(logits, axis=1)
    row_total = jnp.sum(jnp.exp(logits - row_peak[:, None]), axis=1)
    matched = wanted[:, None] == columns[None, :]
    row_hit = jnp.sum(jnp.where(matched, logits, 0.0), axis=1)
    return jnp.stack([row_peak, row_total, row_hit])


def update_weights(prior_weights, clipped, domains, keep):
    weights = prior_weights / jnp.sum(prior_weights)
    batch_rows = clipped.shape[0] // STEPS
    labels = jnp.arange(DOMAINS, dtype=jnp.int32)
    for section_index in range(STEPS):
        row_start = section_index * batch_rows
        block_loss = clipped[row_start : row_start + batch_rows]
        block_keep = keep[row_start : row_start + batch_rows]
        member = (domains[row_start : row_start + batch_rows][:, None] == labels[None, :]).astype(
            jnp.float32
        )
        domain_sum = jnp.dot(block_loss, member, precision=lax.Precision.HIGHEST)
        domain_count = jnp.dot(block_keep, member, precision=lax.Precision.HIGHEST)
        domain_gain = domain_sum / jnp.maximum(domain_count, 1.0)
        raised = weights * jnp.exp(step_size * domain_gain)
        weights = (1.0 - smoothing) * raised / jnp.sum(raised) + smoothing / DOMAINS
    return jnp.log(weights)


def merge_stats(earlier_part, second_part):
    peak_one, total_one, hit_one = earlier_part
    peak_two, total_two, hit_two = second_part
    top_value = jnp.maximum(peak_one, peak_two)
    joined = total_one * jnp.exp(peak_one - top_value) + total_two * jnp.exp(peak_two - top_value)
    return (top_value, joined, hit_one + hit_two)


def local(
    proxy_hidden,
    reference_hidden,
    proxy_head,
    reference_head,
    targets,
    domains,
    keep_mask,
    prior_weights,
):
    all_targets, all_domains, all_keep = gather_turned((targets, domains, keep_mask), DP, (0, 0, 0))
    vocab_dev = proxy_head.shape[0]
    offset = (lax.axis_index(DP) * lax.axis_size("tensor") + lax.axis_index("tensor")) * vocab_dev
    local_target = all_targets - offset
    stacked = jnp.stack([proxy_hidden, reference_hidden])
    full_rows = gather_directly(stacked, "tensor", 2)
    portion = lax.all_gather(full_rows, DP, axis=1, tiled=True)
    proxy_part = row_stats(project(portion[0], proxy_head), local_target)
    reference_part = row_stats(project(portion[1], reference_head), local_target)
    stats = jnp.concatenate([proxy_part, reference_part], axis=0)
    local_peaks = jnp.stack([stats[0], stats[3]])
    local_totals = jnp.stack([stats[1], stats[4]])
    local_hits = jnp.stack([stats[2], stats[5]])
    global_peak, totals, hit_sum = combined_by_axis(
        (local_peaks, local_totals, local_hits), DP_TENSOR, merge_stats
    )
    losses = global_peak + jnp.log(totals) - hit_sum
    keep = all_keep.astype(jnp.float32)
    loss_gap = losses[0] - losses[1]
    excess_all = loss_gap * keep
    clipped = jnp.maximum(loss_gap, 0.0) * keep
    log_weights = update_weights(prior_weights, clipped, all_domains, keep)
    tok_dev = targets.shape[0]
    mine = lax.dynamic_slice_in_dim(excess_all, lax.axis_index(DP) * tok_dev, tok_dev, 0)
    return (mine, log_weights)


def solution(mesh):
    split = Mesh(
        mesh.devices.reshape(4, 4, 2, mesh.shape["tensor"]), ("dp_0", "dp_1", "dp_2", "tensor")
    )
    return jax.shard_map(
        local,
        mesh=split,
        in_specs=(
            P(DP, "tensor"),
            P(DP, "tensor"),
            P(DP_TENSOR, None),
            P(DP_TENSOR, None),
            P(DP),
            P(DP),
            P(DP),
            P(),
        ),
        out_specs=(P(DP), P()),
        check_vma=False,
    )
```

profile of v0, /device:TPU:2, one launch (start us, length us, event | category | flops | bytes accessed | tf_op | source)
XLA Modules:
  0.0 223.1 jit_solution(5851774989392335685)
XLA Ops:
  7.2 0.0 copy-start
  7.2 0.0 copy-start.1
  7.2 0.0 copy-start.2
  7.2 0.0 copy-start.4
  7.2 0.0 all-gather.11.cloned.1.call-start
  7.3 0.8 pad_maximum_fusion
  8.1 0.1 broadcast_in_dim.7
  8.2 31.4 %all_to_all.5 = bf16[8,2,48,512]{3,2,1,0:T(8,128)(2,1)S(1)} all-to-all(bf16[8,2,48,512]{3,2,1,0:T(8,128)(2,1)S(1)} %broadcast_in_dim.7), channel_id=1, replica_groups=mesh['dp_0'=4,'dp_1'=4,'dp_2'=2,'tensor'=8] {'tensor'}, dimensions={0} | all-to-all | bytes 1572864 | tf_op jit(solution)/shard_map/all_to_all | solution.py:31
  39.5 1.0 copy.13
  40.6 0.0 all-gather.11.cloned.1.call-update
  40.6 0.0 copy-done
  40.6 0.0 copy-done.1
  40.6 0.0 copy-done.2
  40.6 24.7 %all-gather.4 = s32[32,48,3]{1,2,0:T(4,128)S(1)} all-gather(s32[1,48,3]{1,2,0:T(4,128)S(1)} %add_bitcast_fusion), channel_id=1, replica_groups=mesh['dp_0'=4,'dp_1'=4,'dp_2'=2,'tensor'=8] {'dp_0','dp_1','dp_2'}, dimensions={0}, use_global_device_ids=true | all-gather | bytes 19008 | tf_op jit(solution)/shard_map/all_gather | solution.py:19
  65.3 0.1 reshape.79
  65.5 0.0 copy-done.4
  65.5 0.6 reduce_sum.76
  66.1 0.3 fusion.9
  66.4 0.3 fusion.5
  66.7 0.3 fusion.13
  67.0 67.0 %all-gather.11.cloned.1.call-done = bf16[2,1536,4096]{2,1,0:T(8,128)(2,1)} async-done(((bf16[2,48,4096]{2,1,0:T(8,128)(2,1)}), bf16[2,1536,4096]{2,1,0:T(8,128)(2,1)}) %all-gather.11.cloned.1.call-update) | async-done | bytes 25165840 | tf_op jit(solution)/shard_map/all_gather | solution.py:127
  134.0 0.0 copy-start.3
  134.0 10.6 %fusion.94 = (f32[1536]{0:T(1024)S(1)}, f32[1536,501]{0,1:T(8,128)S(1)}) fusion(bf16[501,4096]{1,0:T(8,128)(2,1)} %param.10, bf16[2,1536,4096]{2,1,0:T(8,128)(2,1)} %all-gather.11.cloned.1.call-done), kind=kOutput, calls=%fused_computation.175 | convolution fusion | flops 6304806912 | bytes 19795968 | tf_op jit(solution)/shard_map/dot_general | solution.py:72
  144.7 0.0 copy-done.3
  144.7 9.7 %fusion.95 = (f32[1536]{0:T(1024)S(1)}, f32[1536,501]{0,1:T(8,128)S(1)}) fusion(bf16[501,4096]{1,0:T(8,128)(2,1)S(1)} %copy-done.3, bf16[2,1536,4096]{2,1,0:T(8,128)(2,1)} %all-gather.11.cloned.1.call-done), kind=kOutput, calls=%fused_computation.176 | convolution fusion | flops 6304806912 | bytes 19771392 | tf_op jit(solution)/shard_map/dot_general | solution.py:72
  154.4 1.5 select_reduce_fusion
  155.9 0.1 concatenate.17
  156.0 12.4 %all-gather.5 = f32[4,6,1536]{2,1,0:T(8,128)S(1)} all-gather(f32[1,6,1536]{2,1,0:T(8,128)S(1)} %bitcast.371), channel_id=2, replica_groups=mesh['dp_0'=4,'dp_1'=4,'dp_2'=2,'tensor'=8] {'dp_0'}, dimensions={0}, use_global_device_ids=true | all-gather | bytes 184320 | tf_op jit(solution)/shard_map/all_gather | solution.py:53
  168.4 0.1 fusion.61
  168.5 12.1 %all-gather.6 = f32[4,6,1536]{2,1,0:T(8,128)S(1)} all-gather(f32[1,6,1536]{2,1,0:T(8,128)S(1)} %maximum_bitcast_fusion), channel_id=3, replica_groups=mesh['dp_0'=4,'dp_1'=4,'dp_2'=2,'tensor'=8] {'dp_1'}, dimensions={0}, use_global_device_ids=true | all-gather | bytes 184320 | tf_op jit(solution)/shard_map/all_gather | solution.py:53
  180.7 0.1 fusion.51
  180.8 1.9 all-gather.7
  182.7 26.7 %all-gather.8 = f32[8,6,1536]{2,1,0:T(8,128)S(1)} all-gather(f32[1,6,1536]{2,1,0:T(8,128)S(1)} %maximum_bitcast_fusion.2), channel_id=5, replica_groups=mesh['dp_0'=4,'dp_1'=4,'dp_2'=2,'tensor'=8] {'tensor'}, dimensions={0}, use_global_device_ids=true | all-gather | bytes 331776 | tf_op jit(solution)/shard_map/all_gather | solution.py:53
  209.4 0.2 fusion.21
  209.7 0.6 dynamic-slice_multiply_fusion
  210.3 1.6 fusion.96
  211.9 1.6 fusion.97
  213.5 1.6 fusion.98
  215.1 1.2 add_log_fusion
  (21 shorter events, 0.3 us)
Async XLA Ops:
  7.2 33.4 %copy-start = (s32[48]{0:T(128)S(1)}, s32[48]{0:T(128)}, u32[]{:S(2)}) copy-start(s32[48]{0:T(128)} %param.14) | copy-start | bytes 580
  7.2 33.4 %copy-start.1 = (s32[48]{0:T(128)S(1)}, s32[48]{0:T(128)}, u32[]{:S(2)}) copy-start(s32[48]{0:T(128)} %param.13) | copy-start | bytes 580
  7.2 33.4 %copy-start.2 = (s32[48]{0:T(128)S(1)}, s32[48]{0:T(128)}, u32[]{:S(2)}) copy-start(s32[48]{0:T(128)} %param.12) | copy-start | bytes 580
  7.2 58.3 %copy-start.4 = (f32[128]{0:T(128)S(1)}, f32[128]{0:T(128)}, u32[]{:S(2)}) copy-start(f32[128]{0:T(128)} %param.15) | copy-start | bytes 1540
  7.2 126.8 %all-gather.11.cloned.1.call-start = ((), (), s32[]{:S(2)}) async-start(), calls=%async_computation.1 | async-start | bytes 25952256 | tf_op jit(solution)/shard_map/all_gather | solution.py:127
  134.0 10.7 %copy-start.3 = (bf16[501,4096]{1,0:T(8,128)(2,1)S(1)}, bf16[501,4096]{1,0:T(8,128)(2,1)}, u32[]{:S(2)}) copy-start(bf16[501,4096]{1,0:T(8,128)(2,1)} %param.11) | copy-start | bytes 12312580
Sparse Core Ops, SparseCore 0:
  40.7 93.2 all-gather.10
where the time goes:
time: 223 us
  blocking collectives  109 us (49%)
  waiting for transfers between devices  67 us (30%)
  matrix products  26 us (12%)
  between operations  14.3 us (6%)
  other arithmetic  5.31 us (2%)
    all_gather x1, waiting for transfers between devices, local(): portion = lax.all_gather(full_rows, DP, axis=1, tiled=True)  67 us
    all_gather x4, blocking collectives, all_in_one(): both, at, found = (lax.all_gather(jnp.concatenate(lines), axis), 0, {})  53.1 us
    all_to_all x1, blocking collectives, copy_for_each(): return lax.all_to_all(copies, axis, split_axis=0, concat_axis=0, tiled=True)  31.4 us
    all_gather x1, blocking collectives, gather_turned(): whole = lax.all_gather(both, axis, axis=0, tiled=True)  24.7 us
    dot_general x2, matrix products, project(): lax.dot_general(rows, head, (((1,), (1,)), ((), ())), preferred_element_t...  20.3 us
    dot_general x3, matrix products, update_weights(): domain_sum = jnp.dot(block_loss, member, precision=lax.Precision.HIGHEST)  4.82 us
  transfers between devices with their start and end apart: 1, of which 1 were waited for; matrix products, arithmetic and copies ran while one was open for 1% of the time, Pallas kernels for 0%

commit v1 on v0

--- a/solution.py
+++ b/solution.py
@@ -124,7 +124,15 @@
     local_target = all_targets - offset
     stacked = jnp.stack([proxy_hidden, reference_hidden])
     full_rows = gather_directly(stacked, "tensor", 2)
-    portion = lax.all_gather(full_rows, DP, axis=1, tiled=True)
+    portion = jnp.concatenate(
+        lax.all_to_all(
+            jnp.stack([full_rows for _ in range(lax.psum(1, axis_name=DP))], axis=0),
+            axis_name=DP,
+            split_axis=0,
+            concat_axis=0,
+        ),
+        1,
+    )
     proxy_part = row_stats(project(portion[0], proxy_head), local_target)
     reference_part = row_stats(project(portion[1], reference_head), local_target)
     stats = jnp.concatenate([proxy_part, reference_part], axis=0)

time: 223 us -> 565 us (2.53)
  blocking collectives: 109 us -> 508 us
  waiting for transfers between devices: 67 us -> 0.01 us
  local copies, waits for them, and re-layouts: 1.33 us -> 19.2 us
  between operations: 14.3 us -> 0.91 us
  starting transfers between devices: 0.04 us -> 7.82 us
    all_gather x1, blocking collectives: 24.7 us -> 427 us  [gather_turned(): whole = lax.all_gather(both, axis, axis=0, tiled=True)]
    all_gather x1 -> x0, waiting for transfers between devices: 67 us -> none  [local(): portion = lax.all_gather(full_rows, DP, axis=1, tiled=True)]
    slice x0 -> x1, local copies, waits for them, and re-layouts: none -> 10.2 us  [local(): portion[1]]
    another operation x0 -> x2, local copies, waits for them, and re-layouts: none -> 8.64 us  [local(): jnp.stack([full_rows for _ in range(lax.psum(1, axis_name=DP))], axis=0)]
    all_to_all x0 -> x1, starting transfers between devices: none -> 7.82 us  [local(): lax.all_to_all(jnp.stack([full_rows for _ in range(lax.psum(1, axis_name=...]
  transfers between devices with their start and end apart: 1 -> 1, of which waited for: 1 -> 0; matrix products, arithmetic and copies ran while one was open for 1% -> 0% of each run, Pallas kernels for 0% -> 0%
where the time goes in v1:
time: 565 us
  blocking collectives  508 us (90%)
  matrix products  23.4 us (4%)
  local copies, waits for them, and re-layouts  19.2 us (3%)
  starting transfers between devices  7.82 us (1%)
    all_gather x1, blocking collectives, gather_turned(): whole = lax.all_gather(both, axis, axis=0, tiled=True)  427 us
    all_gather x4, blocking collectives, all_in_one(): both, at, found = (lax.all_gather(jnp.concatenate(lines), axis), 0, {})  50 us
    all_to_all x1, blocking collectives, copy_for_each(): return lax.all_to_all(copies, axis, split_axis=0, concat_axis=0, tiled=True)  31.4 us
    dot_general x2, matrix products, project(): lax.dot_general(rows, head, (((1,), (1,)), ((), ())), preferred_element_t...  17.8 us
  transfers between devices with their start and end apart: 1, of which 0 were waited for; matrix products, arithmetic and copies ran while one was open for 0% of the time, Pallas kernels for 0%

profile of v1, /device:TPU:2, one launch (start us, length us, event | category | flops | bytes accessed | tf_op | source)
XLA Modules:
  0.0 565.0 jit_solution(10726857088745858741)
XLA Ops:
  0.6 0.8 pad_maximum_fusion
  1.5 0.1 broadcast_in_dim.7
  1.5 31.4 %all_to_all.10 = bf16[8,2,48,512]{3,2,1,0:T(8,128)(2,1)S(1)} all-to-all(bf16[8,2,48,512]{3,2,1,0:T(8,128)(2,1)S(1)} %broadcast_in_dim.7), channel_id=1, replica_groups=mesh['dp_0'=4,'dp_1'=4,'dp_2'=2,'tensor'=8] {'tensor'}, dimensions={0} | all-to-all | bytes 1572864 | tf_op jit(solution)/shard_map/all_to_all | solution.py:31
  32.9 0.1 copy.13
  33.0 8.6 %stack.36 = bf16[32,2,48,4096]{3,2,1,0:T(8,128)(2,1)} broadcast(bf16[2,48,4096]{2,1,0:T(8,128)(2,1)S(1)} %bitcast.366), dimensions={1,2,3} | broadcast | bytes 25952256 | tf_op jit(solution)/shard_map/stack | solution.py:129
  41.6 0.0 copy-start
  41.6 0.0 copy-start.1
  41.6 0.0 copy-start.2
  41.6 0.0 copy-start.3
  41.6 7.8 %all-to-all-start.1 = ((bf16[32,2,48,4096]{3,2,1,0:T(8,128)(2,1)}), bf16[32,2,48,4096]{3,2,1,0:T(8,128)(2,1)}, u32[]{:S(2)}, u32[]{:S(2)}) async-start(bf16[32,2,48,4096]{3,2,1,0:T(8,128)(2,1)} %stack.36), calls=%async_computation.1 | async-start | bytes 50331648 | tf_op jit(solution)/shard_map/all_to_all | solution.py:128
  49.4 0.0 copy-done
  49.4 0.0 copy-done.1
  49.4 0.0 copy-done.2
  49.5 426.9 %all-gather.4 = s32[32,48,3]{1,2,0:T(4,128)S(1)} all-gather(s32[1,48,3]{1,2,0:T(4,128)S(1)} %add_bitcast_fusion), channel_id=1, replica_groups=mesh['dp_0'=4,'dp_1'=4,'dp_2'=2,'tensor'=8] {'dp_0','dp_1','dp_2'}, dimensions={0}, use_global_device_ids=true | all-gather | bytes 19008 | tf_op jit(solution)/shard_map/all_gather | solution.py:19
  476.4 0.1 reshape.86
  476.5 0.0 copy-done.3
  476.5 0.6 reduce_sum.76
  477.2 0.3 fusion.7
  477.5 0.3 fusion.3
  477.8 0.3 fusion.11
  478.1 0.0 all-to-all-done.1
  478.1 10.2 %fusion.90 = (bf16[1,32,48,4096]{3,2,0,1:T(8,128)(2,1)S(1)}, bf16[1,32,48,4096]{3,2,0,1:T(8,128)(2,1)S(1)}) fusion(bf16[2,32,48,4096]{3,2,0,1:T(8,128)(2,1)} %bitcast.3), kind=kLoop, calls=%fused_computation.169 | loop fusion | bytes 50331648 | tf_op jit(solution)/shard_map/slice | solution.py:137
  488.3 8.9 %fusion.93 = (f32[1536]{0:T(1024)S(1)}, f32[1536,501]{0,1:T(8,128)S(1)}) fusion(bf16[1536,4096]{1,0:T(8,128)(2,1)S(1)} %bitcast.365, bf16[501,4096]{1,0:T(8,128)(2,1)} %param.10), kind=kOutput, calls=%fused_computation.172 | convolution fusion | flops 6304806912 | bytes 19771392 | tf_op jit(solution)/shard_map/dot_general | solution.py:72
  497.2 8.9 %fusion.94 = (f32[1536]{0:T(1024)S(1)}, f32[1536,501]{0,1:T(8,128)S(1)}) fusion(bf16[1536,4096]{1,0:T(8,128)(2,1)S(1)} %bitcast.364, bf16[501,4096]{1,0:T(8,128)(2,1)} %param.11), kind=kOutput, calls=%fused_computation.173 | convolution fusion | flops 6304806912 | bytes 19771392 | tf_op jit(solution)/shard_map/dot_general | solution.py:72
  506.1 1.5 select_reduce_fusion
  507.7 0.1 concatenate.17
  507.7 11.0 %all-gather.5 = f32[4,6,1536]{2,1,0:T(8,128)S(1)} all-gather(f32[1,6,1536]{2,1,0:T(8,128)S(1)} %bitcast.368), channel_id=2, replica_groups=mesh['dp_0'=4,'dp_1'=4,'dp_2'=2,'tensor'=8] {'dp_0'}, dimensions={0}, use_global_device_ids=true | all-gather | bytes 184320 | tf_op jit(solution)/shard_map/all_gather | solution.py:53
  518.8 0.1 fusion.59
  518.9 12.1 %all-gather.6 = f32[4,6,1536]{2,1,0:T(8,128)S(1)} all-gather(f32[1,6,1536]{2,1,0:T(8,128)S(1)} %maximum_bitcast_fusion), channel_id=3, replica_groups=mesh['dp_0'=4,'dp_1'=4,'dp_2'=2,'tensor'=8] {'dp_1'}, dimensions={0}, use_global_device_ids=true | all-gather | bytes 184320 | tf_op jit(solution)/shard_map/all_gather | solution.py:53
  531.0 0.1 fusion.49
  531.1 1.9 all-gather.7
  533.1 25.0 %all-gather.8 = f32[8,6,1536]{2,1,0:T(8,128)S(1)} all-gather(f32[1,6,1536]{2,1,0:T(8,128)S(1)} %maximum_bitcast_fusion.2), channel_id=5, replica_groups=mesh['dp_0'=4,'dp_1'=4,'dp_2'=2,'tensor'=8] {'tensor'}, dimensions={0}, use_global_device_ids=true | all-gather | bytes 331776 | tf_op jit(solution)/shard_map/all_gather | solution.py:53
  558.1 0.2 fusion.19
  558.4 0.6 dynamic-slice_multiply_fusion
  559.0 1.6 fusion.95
  560.6 1.6 fusion.96
  562.2 1.6 fusion.97
  563.8 1.2 add_log_fusion
  (21 shorter events, 0.3 us)
Async XLA Ops:
  41.6 7.8 %copy-start = (s32[48]{0:T(128)S(1)}, s32[48]{0:T(128)}, u32[]{:S(2)}) copy-start(s32[48]{0:T(128)} %param.14) | copy-start | bytes 580
  41.6 7.9 %copy-start.1 = (s32[48]{0:T(128)S(1)}, s32[48]{0:T(128)}, u32[]{:S(2)}) copy-start(s32[48]{0:T(128)} %param.13) | copy-start | bytes 580
  41.6 7.9 %copy-start.2 = (s32[48]{0:T(128)S(1)}, s32[48]{0:T(128)}, u32[]{:S(2)}) copy-start(s32[48]{0:T(128)} %param.12) | copy-start | bytes 580
  41.6 434.9 %copy-start.3 = (f32[128]{0:T(128)S(1)}, f32[128]{0:T(128)}, u32[]{:S(2)}) copy-start(f32[128]{0:T(128)} %param.15) | copy-start | bytes 1540
  41.6 436.5 %all-to-all-start.1 = ((bf16[32,2,48,4096]{3,2,1,0:T(8,128)(2,1)}), bf16[32,2,48,4096]{3,2,1,0:T(8,128)(2,1)}, u32[]{:S(2)}, u32[]{:S(2)}) async-start(bf16[32,2,48,4096]{3,2,1,0:T(8,128)(2,1)} %stack.36), calls=%async_computation.1 | async-start | bytes 50331648 | tf_op jit(solution)/shard_map/all_to_all | solution.py:128
